TPU v7x, 32 devices: a whole 2x2x4 slice. The times are simulated.
32 devices in a mesh: gx: 4 (over y, x), gy: 2 (over core), gz: 4 (over z).
Axes of the slice: x: 2, y: 2, z: 4, core: 2. Of those that a mesh axis runs over, the one named last changes fastest.
Arguments:
- volume: float32 [512, 128, 512], P('gx', 'gy', 'gz'), may hold values from -6 to 6
Outputs:
- prefix: float32 [512, 128, 512], P('gx', 'gy', 'gz')
- box_sum: float32 [512, 128, 512], P('gx', 'gy', 'gz')
All inputs are finite; a program needn't handle non-finite values.
Results may differ from a plain program's by a relative error of at most 0.00055.
Values sent between devices are 32-bit elements; how exact they have to be, the bound alone decides.
A program may use at most 128 MiB of HBM per device.

v0:
```python
import functools
import math

import jax
import jax.numpy as jnp
from jax import lax
from jax.experimental import pallas as pl
from jax.experimental.pallas import tpu as pltpu
from jax.sharding import PartitionSpec as P

F32 = jnp.float32
BF16 = jnp.bfloat16
MESH = pl.DeviceIdType.MESH
USED = (0, 2, 3, 4, 5)
PLANES = 16


def split(a, axis):
    hi = a.astype(BF16)
    lo = (a - hi.astype(F32)).astype(BF16)
    return jnp.concatenate([hi, lo], axis=axis)


def source_index(kind, length):
    return {2: length - 2, 3: length - 1, 4: 0, 5: 1}[kind]


def selector(length):
    kind = lax.broadcasted_iota(jnp.int32, (8, length), 0)
    at = lax.broadcasted_iota(jnp.int32, (8, length), 1)
    pick = kind == 0
    for k in (2, 3, 4, 5):
        pick = pick | ((kind == k) & (at == source_index(k, length)))
    one = jnp.where(pick, 1.0, 0.0).astype(BF16)
    return jnp.concatenate([one, one], axis=1)


def z_sources(rows):
    return lax.dot_general(
        selector(rows.shape[1]),
        split(rows, 1),
        (((1,), (1,)), ((), ())),
        preferred_element_type=F32,
    )


def sources_kernel(ny, nz, v_ref, x_ref, y_ref, z_ref, zy_ref, zx_ref, zxy_ref):
    i, steps = pl.program_id(0), pl.num_programs(0)
    nx = steps * PLANES
    blocks = PLANES * ny // 128
    zrows = z_ref.shape[0] // 8

    @pl.when(i == 0)
    def _():
        x_ref[...] = jnp.zeros_like(x_ref)
        y_ref[...] = jnp.zeros_like(y_ref)
        x_ref[4] = v_ref[pl.ds(0, ny), :]
        x_ref[5] = v_ref[pl.ds(ny, ny), :]

    total = v_ref[pl.ds(0, ny), :]
    for x in range(1, PLANES):
        total = total + v_ref[pl.ds(x * ny, ny), :]
    x_ref[0] = x_ref[0] + total
    at = pl.ds(pl.multiple_of(i * PLANES, PLANES), PLANES)
    y_ref[0, at, :] = jnp.sum(v_ref[...].reshape(PLANES, ny, nz), axis=1)
    for k in (2, 3, 4, 5):
        y_ref[k, at, :] = v_ref[pl.ds(source_index(k, ny), PLANES, stride=ny), :]
    found = z_sources(v_ref[...])
    for b in range(blocks):
        z_ref[pl.ds(i * blocks + b, 8, stride=zrows), :] = found[:, b * 128 : (b + 1) * 128]

    @pl.when(i == steps - 1)
    def _():
        x_ref[2] = v_ref[pl.ds((PLANES - 2) * ny, ny), :]
        x_ref[3] = v_ref[pl.ds((PLANES - 1) * ny, ny), :]
        count = y_ref.shape[1] - 8
        planes = x_ref[...]
        y_ref[0, pl.ds(count, 8), :] = jnp.sum(planes, axis=1)
        for k in (2, 3, 4, 5):
            y_ref[k, pl.ds(count, 8), :] = planes[:, source_index(k, ny), :]
        for k in range(8):
            zy_ref[k] = z_sources(y_ref[k, pl.ds(0, count), :])
        pairs = planes.reshape(4, 2 * ny, nz)
        for k in range(4):
            zx_ref[k] = z_sources(pairs[k])
        corner = y_ref[:, pl.ds(count, 8), :].reshape(64, nz)
        zxy_ref[0] = z_sources(jnp.concatenate([corner, jnp.zeros_like(corner)], axis=0))


class Exchange:
    def __init__(self, send, recv):
        self.send, self.recv, self.count = send, recv, 0

    def start(self, axis, shift, src, dst):
        n, me = lax.axis_size(axis), lax.axis_index(axis)
        at = self.count
        self.count += 1
        copy = pltpu.make_async_remote_copy(
            src_ref=src,
            dst_ref=dst,
            send_sem=self.send.at[at],
            recv_sem=self.recv.at[at],
            device_id={axis: lax.rem(me + shift + n, n)},
            device_id_type=MESH,
        )
        sends = (me + shift >= 0) & (me + shift < n)
        receives = (me - shift >= 0) & (me - shift < n)
        pl.when(sends)(copy.start)
        return sends, receives, copy

    def layers(self, axis, src, carry, halo):
        out = []
        n = lax.axis_size(axis)
        if n > 1:
            out.append(self.start(axis, 1, src.at[pl.ds(2, 2)], halo.at[pl.ds(0, 2)]))
            out.append(self.start(axis, -1, src.at[pl.ds(4, 2)], halo.at[pl.ds(2, 2)]))
        for d in range(1, n):
            out.append(self.start(axis, d, src.at[pl.ds(0, 1)], carry.at[pl.ds(d - 1, 1)]))
        return out

    def whole(self, axis, src, slots):
        n = lax.axis_size(axis)
        out = [self.start(axis, d, src, slots.at[d - 1]) for d in range(1, n)]
        if n > 1:
            out.append(self.start(axis, -1, src, slots.at[n - 1]))
        return out


def arrived(copies):
    for _, receives, copy in copies:
        pl.when(receives)(copy.wait_recv)


def sent(copies):
    for sends, _, copy in copies:
        pl.when(sends)(copy.wait_send)


def carry_total(carry, n):
    total = carry[0]
    for d in range(1, n - 1):
        total = total + carry[d]
    return total


def put_layers(out_ref, carry, halo, n):
    out_ref[0] = carry_total(carry, n)
    out_ref[1] = jnp.zeros_like(out_ref[1])
    for k in range(4):
        out_ref[2 + k] = halo[k]
    for k in (6, 7):
        out_ref[k] = jnp.zeros_like(out_ref[k])


def combined(slots, n, kind):
    total = slots[0]
    for d in range(1, n - 1):
        total = total + slots[d]
    zero = jnp.zeros_like(total)
    result = jnp.where(kind == 0, total, zero)
    result = jnp.where((kind == 2) | (kind == 3), slots[0], result)
    return jnp.where((kind == 4) | (kind == 5), slots[n - 1], result)


def exchange_kernel(
    x_in, y_in, z_in, zy_in, zx_in, zxy_in,
    x_out, y_out, z_out, zy_out, zx_out, zxy_out,
    xc, xh, yc, yh, zc, zh, zyc, zyh, zyk, zxc, zxh, corner_y, corner_x_src, corner_x,
    z1_src, z1, z2_src, z2, send, recv,
):
    sizes = {a: lax.axis_size(a) for a in ("gx", "gy", "gz")}
    nx, ny, nz = sizes["gx"], sizes["gy"], sizes["gz"]
    for ref in (xc, xh, yc, yh, zc, zh, zyc, zyh, zxc, zxh, corner_y, corner_x, z1, z2):
        ref[...] = jnp.zeros_like(ref)
    barrier = pltpu.get_barrier_semaphore()
    for axis, n in sizes.items():
        me = lax.axis_index(axis)
        for d in range(1, n):
            pl.semaphore_signal(
                barrier, inc=1, device_id={axis: lax.rem(me + d, n)}, device_id_type=MESH
            )
    pl.semaphore_wait(barrier, nx + ny + nz - 3)

    ex = Exchange(send, recv)
    to_y = ex.layers("gy", y_in, yc, yh)
    to_y += ex.layers("gy", zy_in, zyc, zyh)
    to_y += ex.whole("gy", zxy_in, corner_y)
    to_x = ex.layers("gx", x_in, xc, xh)
    to_x.append(ex.start("gx", 1, zx_in.at[pl.ds(1, 1)], zxh.at[pl.ds(0, 1)]))
    to_x.append(ex.start("gx", -1, zx_in.at[pl.ds(2, 1)], zxh.at[pl.ds(1, 1)]))
    for d in range(1, nx):
        to_x.append(ex.start("gx", d, zx_in.at[pl.ds(0, 1)], zxc.at[pl.ds(d - 1, 1)]))
    to_z = ex.layers("gz", z_in, zc, zh)

    lane = lax.broadcasted_iota(jnp.int32, (1, 8, 128), 2)
    row = lax.broadcasted_iota(jnp.int32, (1, 8, 128), 1)
    arrived(to_y)
    count = y_in.shape[1] - 8
    put_layers(y_out, yc, yh, ny)
    put_layers(zyk, zyc, zyh, ny)
    z1_src[...] = zyk[...]
    more_z = ex.whole("gz", z1_src, z1)
    corner_x_src[pl.ds(0, 8)] = y_out[:, pl.ds(count, 8), :]
    corner_x_src[pl.ds(8, 1)] = combined(corner_y, ny, lane // 8)
    more_x = ex.whole("gx", corner_x_src, corner_x)

    arrived(to_x)
    put_layers(x_out, xc, xh, nx)
    z2_src[pl.ds(0, 1)] = carry_total(zxc, nx)[None]
    z2_src[pl.ds(1, 2)] = zxh[...]
    z2_src[pl.ds(3, 1)] = jnp.zeros((1, 8, 128), F32)
    arrived(more_x)
    got = corner_x.at[:, pl.ds(0, 8)]
    y_out[:, pl.ds(count, 8), :] = combined(got, nx, row)
    z2_src[pl.ds(4, 1)] = combined(corner_x.at[:, pl.ds(8, 1)], nx, lax.rem(lane, 8))
    last_z = ex.whole("gz", z2_src, z2)

    arrived(to_z)
    put_layers(z_out, zc, zh, nz)
    arrived(more_z)
    zy_out[...] = combined(z1, nz, row)
    arrived(last_z)
    zx_out[...] = combined(z2.at[:, pl.ds(0, 4)], nz, row)
    zxy_out[...] = combined(z2.at[:, pl.ds(4, 1)], nz, row)
    sent(to_y + to_x + to_z + more_z + more_x + last_z)


def z_weights(nz):
    rows = lax.broadcasted_iota(jnp.int32, (nz, nz), 0)
    cols = lax.broadcasted_iota(jnp.int32, (nz, nz), 1)
    lower = jnp.where(rows <= cols, 1.0, 0.0).astype(BF16)
    band = jnp.where(jnp.abs(rows - cols) <= 2, 1.0, 0.0).astype(BF16)
    half = jnp.concatenate([lower, band], axis=1)
    kind = lax.broadcasted_iota(jnp.int32, (8, nz), 0)
    at = lax.broadcasted_iota(jnp.int32, (8, nz), 1)
    add = (kind == 2) & (at == 0)
    add |= (kind == 3) & (at <= 1)
    add |= (kind == 4) & (at >= nz - 2)
    add |= (kind == 5) & (at == nz - 1)
    edge = jnp.concatenate(
        [jnp.where(kind == 0, 1.0, 0.0).astype(BF16), jnp.where(add, 1.0, 0.0).astype(BF16)], axis=1
    )
    return jnp.concatenate([half, half], axis=0), jnp.concatenate([edge, edge], axis=0)


def along_z(rows, edges, w_ref, e_ref):
    main = jnp.dot(split(rows, 1), w_ref[...], preferred_element_type=F32)
    return main + lax.dot_general(
        split(edges, 0), e_ref[...], (((0,), (0,)), ((), ())), preferred_element_type=F32
    )


def final_kernel(
    ny, nz, scale,
    v_ref, x_ref, y_ref, z_ref, zy_ref, zx_ref, zxy_ref, w_ref, e_ref,
    prefix_ref, box_ref,
    grid_z, rows_y, plane_z, run, tall, boxed,
):
    i, steps = pl.program_id(0), pl.num_programs(0)
    count = y_ref.shape[1] - 8
    blocks = PLANES * ny // 128
    zrows = z_ref.shape[0] // 8

    def y_prefix(piece, start):
        row = lax.broadcasted_iota(jnp.int32, (1, 8, nz), 1)
        c = piece.reshape(ny // 8, 8, nz)
        for step in (1, 2, 4):
            c = c + jnp.where(row >= step, pltpu.roll(c, step, 1), 0.0)
        out = []
        for k in range(ny // 8):
            out.append(c[k] + start)
            start = out[-1][7:8]
        return jnp.concatenate(out, axis=0)

    def y_box(slot, piece, before, after):
        tall[slot, pl.ds(8, ny), :] = piece
        tall[slot, pl.ds(6, 1), :] = before[0]
        tall[slot, pl.ds(7, 1), :] = before[1]
        tall[slot, pl.ds(8 + ny, 1), :] = after[0]
        tall[slot, pl.ds(9 + ny, 1), :] = after[1]
        total = piece
        for d in (6, 7, 9, 10):
            total = total + tall[slot, pl.ds(d, ny), :]
        return total

    def row_of(k, x, part):
        return rows_y[k, pl.ds(x, 1), pl.ds(part * nz, nz)]

    @pl.when(i == 0)
    def _():
        for k in USED:
            rows_y[k, pl.ds(0, count), :] = along_z(
                y_ref[k, pl.ds(0, count), :], zy_ref[k], w_ref, e_ref
            )
        corner = along_z(
            y_ref[:, pl.ds(count, 8), :].reshape(64, nz), zxy_ref[0][:, :64], w_ref, e_ref
        )
        rows_y[:, pl.ds(count, 8), :] = corner.reshape(8, 8, 2 * nz)
        edges = jnp.concatenate([zx_ref[k] for k in range(4)], axis=1)
        plane_z[...] = along_z(x_ref[...].reshape(8 * ny, nz), edges, w_ref, e_ref)
        run[...] = y_prefix(plane_z[pl.ds(0, ny), pl.ds(0, nz)], row_of(0, count, 0))
        for k, to in ((2, 0), (3, 1), (4, count + 2), (5, count + 3)):
            boxed[to] = y_box(
                k % 4,
                plane_z[pl.ds(k * ny, ny), pl.ds(nz, nz)],
                [row_of(t, count + k, 1) for t in (2, 3)],
                [row_of(t, count + k, 1) for t in (4, 5)],
            )

    @pl.when(i < steps - 1)
    def _():
        edges = jnp.concatenate(
            [z_ref[pl.ds(i * blocks + b, 8, stride=zrows), :] for b in range(blocks)], axis=1
        )
        grid_z[...] = along_z(v_ref[...], edges, w_ref, e_ref)
        running = run[...]
        here = pl.ds(pl.multiple_of(i * PLANES, PLANES), PLANES)
        starts = rows_y[0, here, pl.ds(0, nz)]
        sides = {t: rows_y[t, here, pl.ds(nz, nz)] for t in (2, 3, 4, 5)}
        for p in range(PLANES):
            x = i * PLANES + p
            at = pl.ds(p * ny, ny)
            running = running + y_prefix(grid_z[at, pl.ds(0, nz)], starts[p : p + 1])
            prefix_ref[at, :] = running * F32(scale)
            boxed[x + 2] = y_box(
                p % 4,
                grid_z[at, pl.ds(nz, nz)],
                [sides[t][p : p + 1] for t in (2, 3)],
                [sides[t][p : p + 1] for t in (4, 5)],
            )
        run[...] = running

    @pl.when(i > 0)
    def _():
        for p in range(PLANES):
            x = (i - 1) * PLANES + p
            total = boxed[x]
            for d in range(1, 5):
                total = total + boxed[x + d]
            box_ref[pl.ds(p * ny, ny), :] = total * F32(1.0 / math.sqrt(125.0))


def fixed(*shape):
    return pl.BlockSpec(shape, lambda i: (0,) * len(shape))


def per_device(volume):
    cx, cy, cz = volume.shape
    nx, ny, nz = (lax.axis_size(a) for a in ("gx", "gy", "gz"))
    steps = cx // PLANES
    rows = PLANES * cy
    zrows = cx * cy // 128
    flat = volume.reshape(cx * cy, cz)

    def of(*shape):
        return jax.ShapeDtypeStruct(shape, F32)

    faces = [(8, cy, cz), (8, cx + 8, cz), (8 * zrows, 128), (8, 8, cx), (4, 8, 2 * cy), (1, 8, 128)]
    x, y, z, zy, zx, zxy = pl.pallas_call(
        functools.partial(sources_kernel, cy, cz),
        grid=(steps,),
        in_specs=[pl.BlockSpec((rows, cz), lambda i: (i, 0))],
        out_specs=[fixed(*s) for s in faces],
        out_shape=[of(*s) for s in faces],
    )(flat)

    z = z.reshape(8, zrows, 128)
    vmem = pl.BlockSpec(memory_space=pltpu.VMEM)
    sent_shapes = [a.shape for a in (x, y, z, zy, zx, zxy)]
    copies = 4 * (nx + ny + nz) + 4
    lx, ly, lz = (max(n - 1, 1) for n in (nx, ny, nz))
    buffers = [
        (lx, cy, cz), (4, cy, cz),
        (ly, cx + 8, cz), (4, cx + 8, cz),
        (lz, zrows, 128), (4, zrows, 128),
        (ly, 8, cx), (4, 8, cx), (8, 8, cx),
        (lx, 8, 128), (2, 8, 128),
        (ny, 1, 8, 128),
        (9, 8, 128), (nx, 9, 8, 128),
        (8, 8, 128), (nz, 8, 8, 128),
        (5, 8, 128), (nz, 5, 8, 128),
    ]
    x, y, z, zy, zx, zxy = pl.pallas_call(
        exchange_kernel,
        in_specs=[vmem] * 6,
        out_specs=[vmem] * 6,
        out_shape=[of(*s) for s in sent_shapes],
        scratch_shapes=[pltpu.VMEM(s, F32) for s in buffers]
        + [pltpu.SemaphoreType.DMA((copies,)), pltpu.SemaphoreType.DMA((copies,))],
        compiler_params=pltpu.CompilerParams(collective_id=0, has_side_effects=True),
    )(x, y, z, zy, zx, zxy)
    z = z.reshape(8 * zrows, 128)

    weights, edge_weights = z_weights(cz)
    scale = 1.0 / math.sqrt(cx * nx * cy * ny * cz * nz)
    prefix, box = pl.pallas_call(
        functools.partial(final_kernel, cy, cz, scale),
        grid=(steps + 1,),
        in_specs=[pl.BlockSpec((rows, cz), lambda i: (jnp.minimum(i, steps - 1), 0))]
        + [fixed(*a.shape) for a in (x, y, z, zy, zx, zxy, weights, edge_weights)],
        out_specs=[
            pl.BlockSpec((rows, cz), lambda i: (jnp.minimum(i, steps - 1), 0)),
            pl.BlockSpec((rows, cz), lambda i: (jnp.maximum(i - 1, 0), 0)),
        ],
        out_shape=[of(cx * cy, cz), of(cx * cy, cz)],
        scratch_shapes=[
            pltpu.VMEM((rows, 2 * cz), F32),
            pltpu.VMEM((8, cx + 8, 2 * cz), F32),
            pltpu.VMEM((8 * cy, 2 * cz), F32),
            pltpu.VMEM((cy, cz), F32),
            pltpu.VMEM((4, cy + 16, cz), F32),
            pltpu.VMEM((cx + 4, cy, cz), F32),
        ],
        compiler_params=pltpu.CompilerParams(vmem_limit_bytes=48 * 1024 * 1024),
    )(flat, x, y, z, zy, zx, zxy, weights, edge_weights)
    return prefix.reshape(cx, cy, cz), box.reshape(cx, cy, cz)


def solution(mesh):
    return jax.shard_map(
        per_device,
        mesh=mesh,
        in_specs=(P("gx", "gy", "gz"),),
        out_specs=(P("gx", "gy", "gz"), P("gx", "gy", "gz")),
        check_vma=False,
    )
```

profile of v0, /device:TPU:0, one launch (start us, length us, event | category | flops | bytes accessed | tf_op | source)
XLA Modules:
  0.0 41.7 jit_solution(9997459587912425063)
XLA Ops:
  0.7 0.1 select_convert_fusion.2
  0.8 0.1 iota.47
  0.9 7.4 %shard_map.30 = (f32[8,64,128]{2,1,0:T(8,128)}, f32[8,136,128]{2,1,0:T(8,128)}, f32[512,128]{1,0:T(8,128)}, f32[8,8,128]{2,1,0:T(8,128)}, f32[4,8,128]{2,1,0:T(8,128)}, /*index=5*/f32[1,8,128]{2,1,0:T(8,128)}) custom-call(f32[8192,128]{1,0:T(8,128)} %bitcast.5), custom_call_target="tpu_custom_call" | custom-call | tf_op jit(solution)/shard_map/pallas_call | solution.py:359
  8.3 17.9 %shard_map.31 = (f32[8,64,128]{2,1,0:T(8,128)}, f32[8,136,128]{2,1,0:T(8,128)}, f32[8,64,128]{2,1,0:T(8,128)}, f32[8,8,128]{2,1,0:T(8,128)}, f32[4,8,128]{2,1,0:T(8,128)}, /*index=5*/f32[1,8,128]{2,1,0:T(8,128)}) custom-call(f32[8,64,128]{2,1,0:T(8,128)} %get-tuple-element.16.x_in, f32[8,136,128]{2,1,0:T(8,128)} %get-tuple-element.17.y_in, ...), custom_call_target="tpu_custom_call" | custom-call | tf_op jit(solution)/shard_map/pallas_call | solution.py:383
  26.2 0.0 copy-start
  26.2 2.2 %copy-done = f32[128,64,128]{2,1,0:T(8,128)S(1)} copy-done((f32[128,64,128]{2,1,0:T(8,128)S(1)}, f32[128,64,128]{2,1,0:T(8,128)}, u32[]{:S(2)}) %copy-start) | copy-done | bytes 4194328
  28.4 0.0 copy-start.1
  28.4 1.1 %copy-done.1 = f32[8,136,128]{2,1,0:T(8,128)S(1)} copy-done((f32[8,136,128]{2,1,0:T(8,128)S(1)}, f32[8,136,128]{2,1,0:T(8,128)}, u32[]{:S(2)}) %copy-start.1) | copy-done | bytes 557080
  29.4 0.0 copy-start.2
  29.4 0.9 %copy-done.2 = f32[8,64,128]{2,1,0:T(8,128)S(1)} copy-done((f32[8,64,128]{2,1,0:T(8,128)S(1)}, f32[8,64,128]{2,1,0:T(8,128)}, u32[]{:S(2)}) %copy-start.2) | copy-done | bytes 262168
  30.4 0.0 copy-start.3
  30.4 0.9 %copy-done.3 = f32[8,64,128]{2,1,0:T(8,128)S(1)} copy-done((f32[8,64,128]{2,1,0:T(8,128)S(1)}, f32[8,64,128]{2,1,0:T(8,128)}, u32[]{:S(2)}) %copy-start.3) | copy-done | bytes 262168
  31.3 0.0 copy-start.4
  31.3 0.8 %copy-done.4 = f32[8,8,128]{2,1,0:T(8,128)S(1)} copy-done((f32[8,8,128]{2,1,0:T(8,128)S(1)}, f32[8,8,128]{2,1,0:T(8,128)}, u32[]{:S(2)}) %copy-start.4) | copy-done | bytes 32792
  32.1 0.0 copy-start.5
  32.1 0.7 %copy-done.5 = f32[4,8,128]{2,1,0:T(8,128)S(1)} copy-done((f32[4,8,128]{2,1,0:T(8,128)S(1)}, f32[4,8,128]{2,1,0:T(8,128)}, u32[]{:S(2)}) %copy-start.5) | copy-done | bytes 16408
  32.8 0.0 copy-start.6
  32.8 0.7 %copy-done.6 = f32[1,8,128]{2,1,0:T(8,128)S(1)} copy-done((f32[1,8,128]{2,1,0:T(8,128)S(1)}, f32[1,8,128]{2,1,0:T(8,128)}, u32[]{:S(2)}) %copy-start.6) | copy-done | bytes 4120
  33.5 8.3 %shard_map.32 = (f32[8192,128]{1,0:T(8,128)}, f32[8192,128]{1,0:T(8,128)}) custom-call(f32[8192,128]{1,0:T(8,128)S(1)} %bitcast.6, f32[8,64,128]{2,1,0:T(8,128)S(1)} %copy-done.2, f32[8,136,128]{2,1,0:T(8,128)S(1)} %copy-done.1, f32[512,128]{1,0:T(8,128)S(1)} %bitcast.7, f32[8,8,128]{2,1,0:T(8,128)S(1)} %copy-done.4, f32[4,8,128]{2,1,0:T(8,128)S(1)} %copy-done.5, ...), custom_call_target="tpu_custom_call" | custom-call | tf_op jit(solution)/shard_map/pallas_call | solution.py:396
  (8 shorter events, 0.1 us)
Async XLA Ops:
  26.2 2.2 %copy-start = (f32[128,64,128]{2,1,0:T(8,128)S(1)}, f32[128,64,128]{2,1,0:T(8,128)}, u32[]{:S(2)}) copy-start(f32[128,64,128]{2,1,0:T(8,128)} %param.1) | copy-start | bytes 12582916
  28.4 1.1 %copy-start.1 = (f32[8,136,128]{2,1,0:T(8,128)S(1)}, f32[8,136,128]{2,1,0:T(8,128)}, u32[]{:S(2)}) copy-start(f32[8,136,128]{2,1,0:T(8,128)} %get-tuple-element.23.y_ref) | copy-start | bytes 1671172
  29.4 0.9 %copy-start.2 = (f32[8,64,128]{2,1,0:T(8,128)S(1)}, f32[8,64,128]{2,1,0:T(8,128)}, u32[]{:S(2)}) copy-start(f32[8,64,128]{2,1,0:T(8,128)} %get-tuple-element.22.x_ref) | copy-start | bytes 786436
  30.4 0.9 %copy-start.3 = (f32[8,64,128]{2,1,0:T(8,128)S(1)}, f32[8,64,128]{2,1,0:T(8,128)}, u32[]{:S(2)}) copy-start(f32[8,64,128]{2,1,0:T(8,128)} %get-tuple-element.24) | copy-start | bytes 786436
  31.3 0.8 %copy-start.4 = (f32[8,8,128]{2,1,0:T(8,128)S(1)}, f32[8,8,128]{2,1,0:T(8,128)}, u32[]{:S(2)}) copy-start(f32[8,8,128]{2,1,0:T(8,128)} %get-tuple-element.25.zy_ref) | copy-start | bytes 98308
  32.1 0.7 %copy-start.5 = (f32[4,8,128]{2,1,0:T(8,128)S(1)}, f32[4,8,128]{2,1,0:T(8,128)}, u32[]{:S(2)}) copy-start(f32[4,8,128]{2,1,0:T(8,128)} %get-tuple-element.26.zx_ref) | copy-start | bytes 49156
  32.8 0.7 %copy-start.6 = (f32[1,8,128]{2,1,0:T(8,128)S(1)}, f32[1,8,128]{2,1,0:T(8,128)}, u32[]{:S(2)}) copy-start(f32[1,8,128]{2,1,0:T(8,128)} %get-tuple-element.27.zxy_ref) | copy-start | bytes 12292
where the time goes:
time: 42.3 us; the launch traced here: 41.7 us
  Pallas kernels  33.5 us (79%)
  local copies, waits for them, and re-layouts  7.36 us (17%)
  between operations  0.7 us (2%)
    pallas_call x1, Pallas kernels, per_device(): pl.pallas_call(exchange_kernel, in_specs=[vmem] * 6, out_specs=[vmem] * 6...  17.9 us
    pallas_call x1, Pallas kernels, per_device(): pl.pallas_call(functools.partial(final_kernel, cy, cz, scale), grid=(step...  8.26 us
    pallas_call x1, Pallas kernels, per_device(): pl.pallas_call(functools.partial(sources_kernel, cy, cz), grid=(steps,),...  7.38 us
    unnamed x14, local copies, waits for them, and re-layouts  7.29 us

commit v1 on v0

--- a/solution.py
+++ b/solution.py
@@ -411,7 +411,7 @@
             pltpu.VMEM((4, cy + 16, cz), F32),
             pltpu.VMEM((cx + 4, cy, cz), F32),
         ],
-        compiler_params=pltpu.CompilerParams(vmem_limit_bytes=48 * 1024 * 1024),
+        compiler_params=pltpu.CompilerParams(vmem_limit_bytes=63 * 1024 * 1024),
     )(flat, x, y, z, zy, zx, zxy, weights, edge_weights)
     return prefix.reshape(cx, cy, cz), box.reshape(cx, cy, cz)
 

time: 42.3 us -> 39.2 us (0.927)
  local copies, waits for them, and re-layouts: 7.36 us -> 0.07 us
  Pallas kernels: 33.5 us -> 36.6 us
  other arithmetic: 0.16 us -> 1.4 us
    unnamed x14 -> x0, local copies, waits for them, and re-layouts: 7.29 us -> none
    pallas_call x1, Pallas kernels: 8.26 us -> 11.3 us  [per_device(): pl.pallas_call(functools.partial(final_kernel, cy, cz, scale), grid=(step...]
    concatenate x1, other arithmetic: 0.01 us -> 0.66 us  [z_weights(): jnp.concatenate([half, half], axis=0)]
    concatenate x1, other arithmetic: 0.01 us -> 0.6 us  [z_weights(): jnp.concatenate([edge, edge], axis=0)]
where the time goes in v1:
time: 39.2 us; the launch traced here: 38.7 us
  Pallas kernels  36.6 us (93%)
  other arithmetic  1.4 us (4%)
  between operations  0.67 us (2%)
    pallas_call x1, Pallas kernels, per_device(): pl.pallas_call(exchange_kernel, in_specs=[vmem] * 6, out_specs=[vmem] * 6...  17.8 us
    pallas_call x1, Pallas kernels, per_device(): pl.pallas_call(functools.partial(final_kernel, cy, cz, scale), grid=(step...  11.3 us
    pallas_call x1, Pallas kernels, per_device(): pl.pallas_call(functools.partial(sources_kernel, cy, cz), grid=(steps,),...  7.37 us

profile of v1, /device:TPU:0, one launch (start us, length us, event | category | flops | bytes accessed | tf_op | source)
XLA Modules:
  0.0 38.7 jit_solution(17934276019216299410)
XLA Ops:
  0.7 0.1 select_convert_fusion.2
  0.8 0.1 iota.47
  0.8 0.6 %maximum_maximum_fusion.1.e_ref = bf16[16,256]{1,0:T(8,128)(2,1)} fusion(bf16[8,128]{1,0:T(8,128)(2,1)S(1)} %select_convert_fusion.2, bf16[8,128]{1,0:T(8,128)(2,1)S(1)} %iota.47), kind=kLoop, calls=%fused_computation.5 | loop fusion | flops 32768 | bytes 12288 | tf_op jit(solution)/shard_map/concatenate | solution.py:243
  1.5 0.7 %maximum_maximum_fusion.w_ref = bf16[256,256]{1,0:T(8,128)(2,1)} fusion(bf16[128,128]{1,0:T(8,128)(2,1)S(1)} %get-tuple-element.30, bf16[128,128]{1,0:T(8,128)(2,1)S(1)} %get-tuple-element.31), kind=kLoop, calls=%fused_computation | loop fusion | flops 524288 | bytes 196608 | tf_op jit(solution)/shard_map/concatenate | solution.py:243
  2.1 7.4 %shard_map.30 = (f32[8,64,128]{2,1,0:T(8,128)}, f32[8,136,128]{2,1,0:T(8,128)}, f32[512,128]{1,0:T(8,128)}, f32[8,8,128]{2,1,0:T(8,128)}, f32[4,8,128]{2,1,0:T(8,128)}, /*index=5*/f32[1,8,128]{2,1,0:T(8,128)}) custom-call(f32[8192,128]{1,0:T(8,128)} %bitcast.5), custom_call_target="tpu_custom_call" | custom-call | tf_op jit(solution)/shard_map/pallas_call | solution.py:359
  9.5 17.8 %shard_map.31 = (f32[8,64,128]{2,1,0:T(8,128)}, f32[8,136,128]{2,1,0:T(8,128)}, f32[8,64,128]{2,1,0:T(8,128)}, f32[8,8,128]{2,1,0:T(8,128)}, f32[4,8,128]{2,1,0:T(8,128)}, /*index=5*/f32[1,8,128]{2,1,0:T(8,128)}) custom-call(f32[8,64,128]{2,1,0:T(8,128)} %get-tuple-element.16.x_in, f32[8,136,128]{2,1,0:T(8,128)} %get-tuple-element.17.y_in, ...), custom_call_target="tpu_custom_call" | custom-call | tf_op jit(solution)/shard_map/pallas_call | solution.py:383
  27.4 11.3 %shard_map.32 = (f32[8192,128]{1,0:T(8,128)}, f32[8192,128]{1,0:T(8,128)}) custom-call(f32[8192,128]{1,0:T(8,128)} %bitcast.6, f32[8,64,128]{2,1,0:T(8,128)} %get-tuple-element.22.x_ref, f32[8,136,128]{2,1,0:T(8,128)} %get-tuple-element.23.y_ref, f32[512,128]{1,0:T(8,128)} %bitcast.7, f32[8,8,128]{2,1,0:T(8,128)} %get-tuple-element.25.zy_ref, ...), custom_call_target="tpu_custom_call" | custom-call | tf_op jit(solution)/shard_map/pallas_call | solution.py:396
  (6 shorter events, 0.1 us)

commit v2 on v1

v2 whole, which is shorter than its diff:
```python
import functools
import math

import jax
import jax.numpy as jnp
from jax import lax
from jax.experimental import pallas as pl
from jax.experimental.pallas import tpu as pltpu
from jax.sharding import PartitionSpec as P

F32 = jnp.float32
BF16 = jnp.bfloat16
MESH = pl.DeviceIdType.MESH
PLANES = 16


def split(a, axis):
    hi = a.astype(BF16)
    lo = (a - hi.astype(F32)).astype(BF16)
    return jnp.concatenate([hi, lo], axis=axis)


def dot(a, b):
    return jnp.dot(a, b, preferred_element_type=F32)


def dot_t(a, b):
    return lax.dot_general(a, b, (((0,), (0,)), ((), ())), preferred_element_type=F32)


def twice(a):
    one = jnp.where(a, 1.0, 0.0).astype(BF16)
    return jnp.concatenate([one, one], axis=0)


def z_weights(nz):
    rows = lax.broadcasted_iota(jnp.int32, (nz, nz), 0)
    cols = lax.broadcasted_iota(jnp.int32, (nz, nz), 1)
    return twice(rows <= cols), twice(jnp.abs(rows - cols) <= 2)


def edge_weights(nz):
    kind = lax.broadcasted_iota(jnp.int32, (8, 2 * nz), 0)
    lane = lax.broadcasted_iota(jnp.int32, (8, 2 * nz), 1)
    at = lane - nz
    add = (kind == 0) & (lane < nz)
    add |= (kind == 1) & (at == 0)
    add |= (kind == 2) & (at >= 0) & (at <= 1)
    add |= (kind == 3) & (at >= nz - 2)
    add |= (kind == 4) & (at == nz - 1)
    return twice(add)


def face_weights(cy):
    row = lax.broadcasted_iota(jnp.int32, (128, 128), 0)
    col = lax.broadcasted_iota(jnp.int32, (128, 128), 1)
    same = row // cy == col // cy
    r, c = row % cy, col % cy
    return [
        twice(same & (r <= c)),
        twice(same),
        twice(same & (jnp.abs(r - c) <= 2)),
        twice(same & (c + cy - r <= 2)),
        twice(same & (r + cy - c <= 2)),
    ]


def y_prefix(piece, start):
    ny, nz = piece.shape
    row = lax.broadcasted_iota(jnp.int32, (1, 8, nz), 1)
    c = piece.reshape(ny // 8, 8, nz)
    for step in (1, 2, 4):
        c = c + jnp.where(row >= step, pltpu.roll(c, step, 1), 0.0)
    out = []
    for k in range(ny // 8):
        out.append(c[k] + start)
        start = out[-1][7:8]
    return jnp.concatenate(out, axis=0)


def y_box(tall, slot, piece, before, after):
    ny = piece.shape[0]
    tall[slot, pl.ds(8, ny), :] = piece
    tall[slot, pl.ds(6, 1), :] = before[0]
    tall[slot, pl.ds(7, 1), :] = before[1]
    tall[slot, pl.ds(8 + ny, 1), :] = after[0]
    tall[slot, pl.ds(9 + ny, 1), :] = after[1]
    total = piece
    for d in (6, 7, 9, 10):
        total = total + tall[slot, pl.ds(d, ny), :]
    return total


class Exchange:
    def __init__(self, send, recv):
        self.send, self.recv, self.count = send, recv, 0

    def start(self, shifts, src, dst):
        at = self.count
        self.count += 1
        device, sends, receives = {}, True, True
        for axis, d in shifts.items():
            n, me = lax.axis_size(axis), lax.axis_index(axis)
            device[axis] = lax.rem(me + d + n, n)
            sends = (me + d >= 0) & (me + d < n) & sends
            receives = (me - d >= 0) & (me - d < n) & receives
        copy = pltpu.make_async_remote_copy(
            src_ref=src,
            dst_ref=dst,
            send_sem=self.send.at[at],
            recv_sem=self.recv.at[at],
            device_id=device,
            device_id_type=MESH,
        )
        pl.when(sends)(copy.start)
        return sends, receives, copy


def arrived(copies):
    for _, receives, copy in copies:
        pl.when(receives)(copy.wait_recv)


def sent(copies):
    for sends, _, copy in copies:
        pl.when(sends)(copy.wait_send)


def total_of(ref):
    total = ref[0]
    for d in range(1, ref.shape[0]):
        total = total + ref[d]
    return total


def sides(n):
    return ((0, 1), (1, -1)) if n > 1 else ()


def exchange_kernel(
    cx, cy, cz, v_hbm,
    yp_out, yb_out, xk_out, xe_out, zk_out,
    v, g, xsrc, ysrc, zraw, zsrc, xzp, xzb,
    yc, yh, zyc, zyh, xc, xh, zc, zh, xzc, xzh, gyc, gyh, tall,
    load, send, recv,
):
    nx, ny, nz = (lax.axis_size(a) for a in ("gx", "gy", "gz"))
    chunk = PLANES * cy
    steps = cx // PLANES
    arows = cx * cy // 128
    per = arows // steps

    def load_of(i):
        at = pl.ds(pl.multiple_of(i * chunk, chunk), chunk)
        return pltpu.make_async_copy(v_hbm.at[at], v.at[at], load.at[i])

    for i in range(steps):
        load_of(i).start()
    for ref in (yc, yh, zyc, zyh, xc, xh, zc, zh, xzc, xzh):
        ref[...] = jnp.zeros_like(ref)
    barrier = pltpu.get_barrier_semaphore()
    peers = 0
    for shifts in [{"gy": d} for d in range(1, ny)] + [
        {"gx": dx, "gz": dz} for dx in range(nx) for dz in range(nz) if dx or dz
    ]:
        device = {a: lax.rem(lax.axis_index(a) + d, lax.axis_size(a)) for a, d in shifts.items()}
        pl.semaphore_signal(barrier, inc=1, device_id=device, device_id_type=MESH)
        peers += 1

    def sources(i, xsum):
        load_of(i).wait()
        base = pl.multiple_of(i * chunk, chunk)
        here = pl.ds(pl.multiple_of(i * PLANES, PLANES), PLANES)
        for p in range(PLANES):
            xsum = xsum + v[pl.ds(base + p * cy, cy), :]
        ysrc[0, here, :] = jnp.sum(v[pl.ds(base, chunk), :].reshape(PLANES, cy, cz), axis=1)
        for k, j in ((1, cy - 2), (2, cy - 1), (3, 0), (4, 1)):
            ysrc[k, here, :] = v[pl.ds(base + j, PLANES, stride=cy), :]
        for b in range(per):
            t = v[pl.ds(base + b * 128, 128), :].T
            row = pl.ds(i * per + b, 1)
            zraw[0, row, :] = jnp.sum(t, axis=0, keepdims=True)
            for k, z in ((1, cz - 2), (2, cz - 1), (3, 0), (4, 1)):
                zraw[k, row, :] = t[z : z + 1]
        return xsum

    xsum = lax.fori_loop(0, steps, sources, jnp.zeros((cy, cz), F32))
    xsrc[0] = xsum
    pl.semaphore_wait(barrier, peers)

    ex = Exchange(send, recv)
    to_y = []
    for s, d in sides(ny):
        to_y.append(ex.start({"gy": d}, ysrc.at[pl.ds(1 + 2 * s, 2)], yh.at[pl.ds(2 * s, 2)]))
        to_y.append(ex.start({"gy": d}, zraw.at[pl.ds(1, 4)], zyh.at[s]))
    for d in range(1, ny):
        to_y.append(ex.start({"gy": d}, ysrc.at[0], yc.at[d - 1]))
        to_y.append(ex.start({"gy": d}, zraw.at[0], zyc.at[d - 1]))

    lower, band = z_weights(cz)
    both = jnp.concatenate([lower, band], axis=1)

    @pl.loop(0, steps)
    def _(i):
        at = pl.ds(pl.multiple_of(i * chunk, chunk), chunk)
        g[at, :] = dot(split(v[at, :], 1), both)

    w_low, w_one, w_band, w_down, w_up = face_weights(cy)
    arrived(to_y)

    ycar = total_of(yc)
    xsrc[0] = y_prefix(xsum, jnp.sum(ycar, axis=0, keepdims=True))
    for q, x in enumerate((cx - 2, cx - 1, 0, 1)):
        rows = [yh[k, pl.ds(x, 1), :] for k in range(4)]
        xsrc[1 + q] = y_box(tall, q, v[pl.ds(x * cy, cy), :], rows[:2], rows[2:])
    zsrc[0] = dot(split(zraw[0], 1), w_low) + dot(split(total_of(zyc), 1), w_one)

    def flat(a):
        return split(a.reshape(4 * arows, 128), 1)

    faces = dot(flat(zraw[pl.ds(1, 4)]), w_band)
    faces = faces + dot(flat(zyh[0]), w_down) + dot(flat(zyh[1]), w_up)
    zsrc[pl.ds(1, 4)] = faces.reshape(4, arows, 128)
    line = jnp.sum(zsrc[0], axis=0, keepdims=True)
    whole = line
    for p in range(1, 128 // cy):
        whole = whole + pltpu.roll(line, p * cy, 1)
    xzp[...] = jnp.broadcast_to(whole, (8, 128))
    for s, a in ((0, arows - 1), (1, 0)):
        for k in range(4):
            xzb[2 * s + k // 2, pl.ds(k % 2, 1), :] = zsrc[1 + k, pl.ds(a, 1), :]

    rest = []
    for s, d in sides(nz):
        rest.append(ex.start({"gz": d}, zsrc.at[pl.ds(1 + 2 * s, 2)], zh.at[pl.ds(2 * s, 2)]))
    for d in range(1, nz):
        rest.append(ex.start({"gz": d}, zsrc.at[0], zc.at[d - 1]))
    for s, d in sides(nx):
        rest.append(ex.start({"gx": d}, xsrc.at[pl.ds(1 + 2 * s, 2)], xh.at[pl.ds(2 * s, 2)]))
    for d in range(1, nx):
        rest.append(ex.start({"gx": d}, xsrc.at[0], xc.at[d - 1]))
    for s, d in sides(nx):
        for t, e in sides(nz):
            at = 2 * s + t
            rest.append(ex.start({"gx": d, "gz": e}, xzb.at[at], xzh.at[at]))
    for d in range(1, nx):
        for e in range(1, nz):
            at = (d - 1) * (nz - 1) + e - 1
            rest.append(ex.start({"gx": d, "gz": e}, xzp, xzc.at[at]))

    gyc[...] = dot(split(ycar, 1), lower)
    gyh[...] = dot(split(yh[...].reshape(4 * cx, cz), 1), band).reshape(4, cx, cz)

    @pl.loop(0, steps)
    def _(i):
        here = pl.ds(pl.multiple_of(i * PLANES, PLANES), PLANES)
        starts = gyc[here, :]
        ends = [gyh[k, here, :] for k in range(4)]
        for p in range(PLANES):
            at = pl.ds(pl.multiple_of(i * chunk, chunk) + p * cy, cy)
            rows = [e[p : p + 1] for e in ends]
            yp_out[at, :] = y_prefix(g[at, pl.ds(0, cz)], starts[p : p + 1])
            yb_out[at, :] = y_box(tall, p % 4, g[at, pl.ds(cz, cz)], rows[:2], rows[2:])

    arrived(rest)
    xk_out[0] = total_of(xc)
    xk_out[pl.ds(1, 4)] = xh[...]
    zero = jnp.zeros((8, 128), F32)
    row = lax.broadcasted_iota(jnp.int32, (8, 128), 0)
    xe_out[0] = jnp.where(row == 0, total_of(xzc), zero)
    for s in range(2):
        low, high = pltpu.roll(xzh[2 * s], 1, 0), pltpu.roll(xzh[2 * s + 1], 3, 0)
        inside = jnp.where((row == 1) | (row == 2), low, zero)
        xe_out[1 + s] = jnp.where((row == 3) | (row == 4), high, inside)
    zk_out[...] = jnp.zeros_like(zk_out)
    zk_out[0, pl.ds(0, arows), :] = total_of(zc)
    zk_out[pl.ds(1, 4), pl.ds(0, arows), :] = zh[...]
    sent(to_y + rest)


def final_kernel(
    cx, cy, cz, scale, yp, yb, xk, xe, zk, prefix_hbm, box_hbm, mm, prefix, box, psem, bsem
):
    chunk = PLANES * cy
    steps = cx // PLANES
    arows = cx * cy // 128
    per = arows // steps
    pad = zk.shape[0] // 8
    box_scale = F32(1.0 / math.sqrt(125.0))
    edge = edge_weights(cz)
    lower, band = z_weights(cz)

    outer = dot_t(split(jnp.concatenate([xe[0], xe[1], xe[2]], axis=1), 0), edge)
    running = dot(split(xk[0], 1), lower) + outer[:cy, :cz]
    halo = dot(split(xk[pl.ds(1, 4)].reshape(4 * cy, cz), 1), band) + outer[128 : 128 + 4 * cy, cz:]
    halo = [halo[k * cy : (k + 1) * cy] for k in range(4)]

    def put(src, dst, sem):
        copy = pltpu.make_async_copy(src, dst, sem)
        copy.start()
        return copy

    copies = []
    window = halo[:2]
    for i in range(steps):
        slot = i % 2
        tiles = [zk[pl.ds(i * per + b, 8, stride=pad), :] for b in range(per)]
        mm[slot] = dot_t(split(jnp.concatenate(tiles, axis=1), 0), edge)
        for p in range(PLANES):
            x = i * PLANES + p
            at, here = pl.ds(x * cy, cy), pl.ds(p * cy, cy)
            running = running + (yp[at, :] + mm[slot, here, pl.ds(0, cz)])
            prefix[at, :] = running * F32(scale)
            window.append(yb[at, :] + mm[slot, here, pl.ds(cz, cz)])
            if len(window) == 5:
                total = (window[0] + window[1]) + (window[2] + window[3]) + window[4]
                box[pl.ds((x - 2) * cy, cy), :] = total * box_scale
                window = window[1:]
        at = pl.ds(i * chunk, chunk)
        copies.append(put(prefix.at[at], prefix_hbm.at[at], psem.at[i]))
        first = max(i * PLANES - 2, 0)
        at = pl.ds(first * cy, ((i + 1) * PLANES - 2 - first) * cy)
        copies.append(put(box.at[at], box_hbm.at[at], bsem.at[i]))
    for k in (2, 3):
        window.append(halo[k])
        total = (window[0] + window[1]) + (window[2] + window[3]) + window[4]
        box[pl.ds((cx - 4 + k) * cy, cy), :] = total * box_scale
        window = window[1:]
    at = pl.ds((cx - 2) * cy, 2 * cy)
    copies.append(put(box.at[at], box_hbm.at[at], bsem.at[steps]))
    for copy in copies:
        copy.wait()


def per_device(volume):
    cx, cy, cz = volume.shape
    nx, ny, nz = (lax.axis_size(a) for a in ("gx", "gy", "gz"))
    steps = cx // PLANES
    rows = cx * cy
    arows = rows // 128
    lx, ly, lz = (max(n - 1, 1) for n in (nx, ny, nz))
    copies = 4 + 2 * ly + 2 + lz + 2 + lx + 4 + lx * lz
    vmem = pl.BlockSpec(memory_space=pltpu.VMEM)
    hbm = pl.BlockSpec(memory_space=pltpu.HBM)
    flat = pltpu.with_memory_space_constraint(volume.reshape(rows, cz), pltpu.HBM)

    outs = [(rows, cz), (rows, cz), (5, cy, cz), (3, 8, 128), (8, arows + 8, 128)]
    buffers = [
        (rows, cz), (rows, 2 * cz), (5, cy, cz), (5, cx, cz),
        (5, arows, 128), (5, arows, 128), (8, 128), (4, 8, 128),
        (ly, cx, cz), (4, cx, cz), (ly, arows, 128), (2, 4, arows, 128),
        (lx, cy, cz), (4, cy, cz), (lz, arows, 128), (4, arows, 128),
        (lx * lz, 8, 128), (4, 8, 128), (cx, cz), (4, cx, cz), (4, cy + 16, cz),
    ]
    yp, yb, xk, xe, zk = pl.pallas_call(
        functools.partial(exchange_kernel, cx, cy, cz),
        in_specs=[hbm],
        out_specs=[vmem] * len(outs),
        out_shape=[pltpu.VMEM(s, F32) for s in outs],
        scratch_shapes=[pltpu.VMEM(s, F32) for s in buffers]
        + [
            pltpu.SemaphoreType.DMA((steps,)),
            pltpu.SemaphoreType.DMA((copies,)),
            pltpu.SemaphoreType.DMA((copies,)),
        ],
        compiler_params=pltpu.CompilerParams(
            collective_id=0, has_side_effects=True, vmem_limit_bytes=40 * 1024 * 1024
        ),
    )(flat)

    scale = 1.0 / math.sqrt(cx * nx * cy * ny * cz * nz)
    prefix, box = pl.pallas_call(
        functools.partial(final_kernel, cx, cy, cz, scale),
        in_specs=[vmem] * 5,
        out_specs=[hbm] * 2,
        out_shape=[jax.ShapeDtypeStruct((rows, cz), F32)] * 2,
        scratch_shapes=[
            pltpu.VMEM((2, PLANES * cy, 2 * cz), F32),
            pltpu.VMEM((rows, cz), F32),
            pltpu.VMEM((rows, cz), F32),
            pltpu.SemaphoreType.DMA((steps,)),
            pltpu.SemaphoreType.DMA((steps + 1,)),
        ],
        compiler_params=pltpu.CompilerParams(vmem_limit_bytes=40 * 1024 * 1024),
    )(yp, yb, xk, xe, zk.reshape(8 * (arows + 8), 128))
    return prefix.reshape(cx, cy, cz), box.reshape(cx, cy, cz)


def solution(mesh):
    return jax.shard_map(
        per_device,
        mesh=mesh,
        in_specs=(P("gx", "gy", "gz"),),
        out_specs=(P("gx", "gy", "gz"), P("gx", "gy", "gz")),
        check_vma=False,
    )
```

time: 39.2 us -> 19.9 us (0.51)
  Pallas kernels: 36.6 us -> 19.1 us
  other arithmetic: 1.4 us -> 0 us
    pallas_call x3 -> x2, Pallas kernels: 36.6 us -> 19.1 us  [the longest x1 15.1 us: per_device(): pl.pallas_call(functools.partial(exchange_kernel, cx, cy, cz), in_specs=[...]
    concatenate x2 -> x0, other arithmetic: 1.26 us -> none  [the longest x1 0.66 us: z_weights(): jnp.concatenate([half, half], axis=0)]
where the time goes in v2:
time: 19.9 us; the launch traced here: 19.7 us
  Pallas kernels  19.1 us (96%)
  between operations  0.64 us (3%)
    pallas_call x1, Pallas kernels, per_device(): pl.pallas_call(functools.partial(exchange_kernel, cx, cy, cz), in_specs=[...  15.1 us
    pallas_call x1, Pallas kernels, per_device(): pl.pallas_call(functools.partial(final_kernel, cx, cy, cz, scale), in_spe...  3.97 us

profile of v2, /device:TPU:0, one launch (start us, length us, event | category | flops | bytes accessed | tf_op | source)
XLA Modules:
  0.0 19.7 jit_solution(1857694539249983395)
XLA Ops:
  0.6 15.1 %shard_map.30 = (f32[8192,128]{1,0:T(8,128)S(1)}, f32[8192,128]{1,0:T(8,128)S(1)}, f32[5,64,128]{2,1,0:T(8,128)S(1)}, f32[3,8,128]{2,1,0:T(8,128)S(1)}, f32[8,72,128]{2,1,0:T(8,128)S(1)}) custom-call(f32[8192,128]{1,0:T(8,128)} %bitcast.5), custom_call_target="tpu_custom_call" | custom-call | tf_op jit(solution)/shard_map/pallas_call | solution.py:355
  15.8 4.0 %shard_map.31 = (f32[8192,128]{1,0:T(8,128)}, f32[8192,128]{1,0:T(8,128)}) custom-call(f32[8192,128]{1,0:T(8,128)S(1)} %get-tuple-element.9.yp, f32[8192,128]{1,0:T(8,128)S(1)} %get-tuple-element.10.yb, f32[5,64,128]{2,1,0:T(8,128)S(1)} %get-tuple-element.11.xk, f32[3,8,128]{2,1,0:T(8,128)S(1)} %get-tuple-element.12.xe, f32[576,128]{1,0:T(8,128)S(1)} %bitcast.4), custom_call_target="tpu_custom_call" | custom-call | tf_op jit(solution)/shard_map/pallas_call | solution.py:372

commit v3 on v2

--- a/solution.py
+++ b/solution.py
@@ -95,7 +95,7 @@
     def __init__(self, send, recv):
         self.send, self.recv, self.count = send, recv, 0
 
-    def start(self, shifts, src, dst):
+    def start(self, shifts, src, dst, step=0):
         at = self.count
         self.count += 1
         device, sends, receives = {}, True, True
@@ -104,6 +104,9 @@
             device[axis] = lax.rem(me + d + n, n)
             sends = (me + d >= 0) & (me + d < n) & sends
             receives = (me - d >= 0) & (me - d < n) & receives
+            if step:
+                sends &= lax.rem(me, 2 * step) == step - 1
+                receives &= lax.rem(me - d + n, 2 * step) == step - 1
         copy = pltpu.make_async_remote_copy(
             src_ref=src,
             dst_ref=dst,
@@ -126,11 +129,15 @@
         pl.when(sends)(copy.wait_send)
 
 
-def total_of(ref):
+def total_of(ref, count=None):
     total = ref[0]
-    for d in range(1, ref.shape[0]):
+    for d in range(1, count or ref.shape[0]):
         total = total + ref[d]
     return total
+
+
+def doublings(n):
+    return [1 << k for k in range((n - 1).bit_length())]
 
 
 def sides(n):
@@ -141,7 +148,7 @@
     cx, cy, cz, v_hbm,
     yp_out, yb_out, xk_out, xe_out, zk_out,
     v, g, xsrc, ysrc, zraw, zsrc, xzp, xzb,
-    yc, yh, zyc, zyh, xc, xh, zc, zh, xzc, xzh, gyc, gyh, tall,
+    yc, yh, zyc, zyh, xc, xh, zc, zh, xzc, xzh, q, zfw, qfw, gyc, gyh, tall,
     load, send, recv,
 ):
     nx, ny, nz = (lax.axis_size(a) for a in ("gx", "gy", "gz"))
@@ -156,16 +163,26 @@
 
     for i in range(steps):
         load_of(i).start()
-    for ref in (yc, yh, zyc, zyh, xc, xh, zc, zh, xzc, xzh):
+    for ref in (yc, yh, zyc, zyh, xc, xh, zc, zh, xzc, xzh, q):
         ref[...] = jnp.zeros_like(ref)
     barrier = pltpu.get_barrier_semaphore()
+    near = [{"gy": d} for d in range(1, ny)] + [{"gx": d} for d in range(1, nx)]
+    near += [{"gz": d} for d in range(1, doublings(nz)[-1] + 1 if nz > 1 else 1)]
+    near += [{"gx": d, "gz": e} for _, d in sides(nx) for _, e in sides(nz) if d > 0]
     peers = 0
-    for shifts in [{"gy": d} for d in range(1, ny)] + [
-        {"gx": dx, "gz": dz} for dx in range(nx) for dz in range(nz) if dx or dz
-    ]:
-        device = {a: lax.rem(lax.axis_index(a) + d, lax.axis_size(a)) for a, d in shifts.items()}
-        pl.semaphore_signal(barrier, inc=1, device_id=device, device_id_type=MESH)
-        peers += 1
+    for shifts in near:
+        for sign in (1, -1):
+            there, device = True, {}
+            for axis, d in shifts.items():
+                to, n = lax.axis_index(axis) + sign * d, lax.axis_size(axis)
+                there = (to >= 0) & (to < n) & there
+                device[axis] = lax.rem(to + n, n)
+
+            @pl.when(there)
+            def _():
+                pl.semaphore_signal(barrier, inc=1, device_id=device, device_id_type=MESH)
+
+            peers = peers + there.astype(jnp.int32)
 
     def sources(i, xsum):
         load_of(i).wait()
@@ -200,19 +217,20 @@
     lower, band = z_weights(cz)
     both = jnp.concatenate([lower, band], axis=1)
 
-    @pl.loop(0, steps)
-    def _(i):
+    def along_z(i):
         at = pl.ds(pl.multiple_of(i * chunk, chunk), chunk)
         g[at, :] = dot(split(v[at, :], 1), both)
 
+    early = steps // 2
+    pl.loop(0, early)(along_z)
     w_low, w_one, w_band, w_down, w_up = face_weights(cy)
     arrived(to_y)
 
     ycar = total_of(yc)
     xsrc[0] = y_prefix(xsum, jnp.sum(ycar, axis=0, keepdims=True))
-    for q, x in enumerate((cx - 2, cx - 1, 0, 1)):
-        rows = [yh[k, pl.ds(x, 1), :] for k in range(4)]
-        xsrc[1 + q] = y_box(tall, q, v[pl.ds(x * cy, cy), :], rows[:2], rows[2:])
+    for k, x in enumerate((cx - 2, cx - 1, 0, 1)):
+        rows = [yh[b, pl.ds(x, 1), :] for b in range(4)]
+        xsrc[1 + k] = y_box(tall, k, v[pl.ds(x * cy, cy), :], rows[:2], rows[2:])
     zsrc[0] = dot(split(zraw[0], 1), w_low) + dot(split(total_of(zyc), 1), w_one)
 
     def flat(a):
@@ -230,11 +248,18 @@
         for k in range(4):
             xzb[2 * s + k // 2, pl.ds(k % 2, 1), :] = zsrc[1 + k, pl.ds(a, 1), :]
 
-    rest = []
+    steps_z = doublings(nz)
+
+    def pass_on(k, src, slots):
+        step = steps_z[k]
+        return [ex.start({"gz": d}, src, slots.at[k], step) for d in range(1, step + 1)]
+
+    lines = [ex.start({"gx": d}, xzp, xzc.at[d - 1]) for d in range(1, nx)]
+    rest, carries, ends = [], [], []
+    if steps_z:
+        carries.append(pass_on(0, zsrc.at[0], zc))
     for s, d in sides(nz):
         rest.append(ex.start({"gz": d}, zsrc.at[pl.ds(1 + 2 * s, 2)], zh.at[pl.ds(2 * s, 2)]))
-    for d in range(1, nz):
-        rest.append(ex.start({"gz": d}, zsrc.at[0], zc.at[d - 1]))
     for s, d in sides(nx):
         rest.append(ex.start({"gx": d}, xsrc.at[pl.ds(1 + 2 * s, 2)], xh.at[pl.ds(2 * s, 2)]))
     for d in range(1, nx):
@@ -243,31 +268,46 @@
         for t, e in sides(nz):
             at = 2 * s + t
             rest.append(ex.start({"gx": d, "gz": e}, xzb.at[at], xzh.at[at]))
-    for d in range(1, nx):
-        for e in range(1, nz):
-            at = (d - 1) * (nz - 1) + e - 1
-            rest.append(ex.start({"gx": d, "gz": e}, xzp, xzc.at[at]))
+
+    def forward_carry(k):
+        arrived(carries[-1])
+        zfw[k] = zsrc[0] + total_of(zc, k)
+        carries.append(pass_on(k, zfw.at[k], zc))
+
+    def forward_line(k):
+        arrived(ends[-1] if k else lines)
+        qfw[k] = total_of(xzc) + (total_of(q, k) if k else 0.0)
+        ends.append(pass_on(k, qfw.at[k], q))
 
     gyc[...] = dot(split(ycar, 1), lower)
     gyh[...] = dot(split(yh[...].reshape(4 * cx, cz), 1), band).reshape(4, cx, cz)
 
-    @pl.loop(0, steps)
-    def _(i):
+    def along_y(i):
         here = pl.ds(pl.multiple_of(i * PLANES, PLANES), PLANES)
         starts = gyc[here, :]
-        ends = [gyh[k, here, :] for k in range(4)]
+        beyond = [gyh[k, here, :] for k in range(4)]
         for p in range(PLANES):
             at = pl.ds(pl.multiple_of(i * chunk, chunk) + p * cy, cy)
-            rows = [e[p : p + 1] for e in ends]
+            rows = [e[p : p + 1] for e in beyond]
             yp_out[at, :] = y_prefix(g[at, pl.ds(0, cz)], starts[p : p + 1])
             yb_out[at, :] = y_box(tall, p % 4, g[at, pl.ds(cz, cz)], rows[:2], rows[2:])
 
-    arrived(rest)
+    work = [functools.partial(pl.loop(early, steps), along_z)]
+    work += [functools.partial(pl.loop(i, i + 2), along_y) for i in range(0, steps, 2)]
+    jobs = [functools.partial(forward_carry, k) for k in range(1, len(steps_z))]
+    jobs += [functools.partial(forward_line, k) for k in range(len(steps_z))]
+    while work or jobs:
+        if work:
+            work.pop(0)()
+        if jobs and len(work) < 4:
+            jobs.pop(0)()
+
+    arrived(rest + sum(carries[-1:] + ends[-1:], []))
     xk_out[0] = total_of(xc)
     xk_out[pl.ds(1, 4)] = xh[...]
     zero = jnp.zeros((8, 128), F32)
     row = lax.broadcasted_iota(jnp.int32, (8, 128), 0)
-    xe_out[0] = jnp.where(row == 0, total_of(xzc), zero)
+    xe_out[0] = jnp.where(row == 0, total_of(q), zero)
     for s in range(2):
         low, high = pltpu.roll(xzh[2 * s], 1, 0), pltpu.roll(xzh[2 * s + 1], 3, 0)
         inside = jnp.where((row == 1) | (row == 2), low, zero)
@@ -275,7 +315,7 @@
     zk_out[...] = jnp.zeros_like(zk_out)
     zk_out[0, pl.ds(0, arows), :] = total_of(zc)
     zk_out[pl.ds(1, 4), pl.ds(0, arows), :] = zh[...]
-    sent(to_y + rest)
+    sent(to_y + lines + rest + sum(carries + ends, []))
 
 
 def final_kernel(
@@ -338,8 +378,9 @@
     steps = cx // PLANES
     rows = cx * cy
     arows = rows // 128
-    lx, ly, lz = (max(n - 1, 1) for n in (nx, ny, nz))
-    copies = 4 + 2 * ly + 2 + lz + 2 + lx + 4 + lx * lz
+    lx, ly = (max(n - 1, 1) for n in (nx, ny))
+    lz = max(len(doublings(nz)), 1)
+    copies = 4 + 2 * ly + 2 + 2 + lx + 4 + lx + 2 * nz
     vmem = pl.BlockSpec(memory_space=pltpu.VMEM)
     hbm = pl.BlockSpec(memory_space=pltpu.HBM)
     flat = pltpu.with_memory_space_constraint(volume.reshape(rows, cz), pltpu.HBM)
@@ -350,7 +391,7 @@
         (5, arows, 128), (5, arows, 128), (8, 128), (4, 8, 128),
         (ly, cx, cz), (4, cx, cz), (ly, arows, 128), (2, 4, arows, 128),
         (lx, cy, cz), (4, cy, cz), (lz, arows, 128), (4, arows, 128),
-        (lx * lz, 8, 128), (4, 8, 128), (cx, cz), (4, cx, cz), (4, cy + 16, cz),
+        (lx, 8, 128), (4, 8, 128), (lz, 8, 128), (lz, arows, 128), (lz, 8, 128), (cx, cz), (4, cx, cz), (4, cy + 16, cz),
     ]
     yp, yb, xk, xe, zk = pl.pallas_call(
         functools.partial(exchange_kernel, cx, cy, cz),

time: 19.9 us -> 17.7 us (0.89)
  Pallas kernels: 19.1 us -> 16.9 us
    pallas_call x1, Pallas kernels: 15.1 us -> 12.9 us  [per_device(): pl.pallas_call(functools.partial(exchange_kernel, cx, cy, cz), in_specs=[...]
where the time goes in v3:
time: 17.7 us; the launch traced here: 17.5 us
  Pallas kernels  16.9 us (95%)
  between operations  0.64 us (4%)
    pallas_call x1, Pallas kernels, per_device(): pl.pallas_call(functools.partial(exchange_kernel, cx, cy, cz), in_specs=[...  12.9 us
    pallas_call x1, Pallas kernels, per_device(): pl.pallas_call(functools.partial(final_kernel, cx, cy, cz, scale), in_spe...  3.97 us

profile of v3, /device:TPU:0, one launch (start us, length us, event | category | flops | bytes accessed | tf_op | source)
XLA Modules:
  0.0 17.5 jit_solution(16649240020172434061)
XLA Ops:
  0.6 12.9 %shard_map.30 = (f32[8192,128]{1,0:T(8,128)S(1)}, f32[8192,128]{1,0:T(8,128)S(1)}, f32[5,64,128]{2,1,0:T(8,128)S(1)}, f32[3,8,128]{2,1,0:T(8,128)S(1)}, f32[8,72,128]{2,1,0:T(8,128)S(1)}) custom-call(f32[8192,128]{1,0:T(8,128)} %bitcast.5), custom_call_target="tpu_custom_call" | custom-call | tf_op jit(solution)/shard_map/pallas_call | solution.py:396
  13.6 4.0 %shard_map.31 = (f32[8192,128]{1,0:T(8,128)}, f32[8192,128]{1,0:T(8,128)}) custom-call(f32[8192,128]{1,0:T(8,128)S(1)} %get-tuple-element.9.yp, f32[8192,128]{1,0:T(8,128)S(1)} %get-tuple-element.10.yb, f32[5,64,128]{2,1,0:T(8,128)S(1)} %get-tuple-element.11.xk, f32[3,8,128]{2,1,0:T(8,128)S(1)} %get-tuple-element.12.xe, f32[576,128]{1,0:T(8,128)S(1)} %bitcast.4), custom_call_target="tpu_custom_call" | custom-call | tf_op jit(solution)/shard_map/pallas_call | solution.py:413

commit v4 on v3

--- a/solution.py
+++ b/solution.py
@@ -12,6 +12,7 @@
 BF16 = jnp.bfloat16
 MESH = pl.DeviceIdType.MESH
 PLANES = 16
+EARLY = 2
 
 
 def split(a, axis):
@@ -148,7 +149,7 @@
     cx, cy, cz, v_hbm,
     yp_out, yb_out, xk_out, xe_out, zk_out,
     v, g, xsrc, ysrc, zraw, zsrc, xzp, xzb,
-    yc, yh, zyc, zyh, xc, xh, zc, zh, xzc, xzh, q, zfw, qfw, gyc, gyh, tall,
+    yc, yh, zyc, zyh, xc, xh, zc, zh, xzc, xzh, q, zfw, qfw, gyc, gyh, tall, w, fw,
     load, send, recv,
 ):
     nx, ny, nz = (lax.axis_size(a) for a in ("gx", "gy", "gz"))
@@ -184,6 +185,10 @@
 
             peers = peers + there.astype(jnp.int32)
 
+    w[...] = jnp.concatenate(z_weights(cz), axis=1)
+    for k, weight in enumerate(face_weights(cy)):
+        fw[k] = weight
+
     def sources(i, xsum):
         load_of(i).wait()
         base = pl.multiple_of(i * chunk, chunk)
@@ -214,23 +219,16 @@
         to_y.append(ex.start({"gy": d}, ysrc.at[0], yc.at[d - 1]))
         to_y.append(ex.start({"gy": d}, zraw.at[0], zyc.at[d - 1]))
 
-    lower, band = z_weights(cz)
-    both = jnp.concatenate([lower, band], axis=1)
-
     def along_z(i):
         at = pl.ds(pl.multiple_of(i * chunk, chunk), chunk)
-        g[at, :] = dot(split(v[at, :], 1), both)
-
-    early = steps // 2
+        g[at, :] = dot(split(v[at, :], 1), w[...])
+
+    early = EARLY
     pl.loop(0, early)(along_z)
-    w_low, w_one, w_band, w_down, w_up = face_weights(cy)
+    w_low, w_one, w_band, w_down, w_up = (fw[k] for k in range(5))
     arrived(to_y)
 
     ycar = total_of(yc)
-    xsrc[0] = y_prefix(xsum, jnp.sum(ycar, axis=0, keepdims=True))
-    for k, x in enumerate((cx - 2, cx - 1, 0, 1)):
-        rows = [yh[b, pl.ds(x, 1), :] for b in range(4)]
-        xsrc[1 + k] = y_box(tall, k, v[pl.ds(x * cy, cy), :], rows[:2], rows[2:])
     zsrc[0] = dot(split(zraw[0], 1), w_low) + dot(split(total_of(zyc), 1), w_one)
 
     def flat(a):
@@ -260,6 +258,10 @@
         carries.append(pass_on(0, zsrc.at[0], zc))
     for s, d in sides(nz):
         rest.append(ex.start({"gz": d}, zsrc.at[pl.ds(1 + 2 * s, 2)], zh.at[pl.ds(2 * s, 2)]))
+    xsrc[0] = y_prefix(xsum, jnp.sum(ycar, axis=0, keepdims=True))
+    for k, x in enumerate((cx - 2, cx - 1, 0, 1)):
+        rows = [yh[b, pl.ds(x, 1), :] for b in range(4)]
+        xsrc[1 + k] = y_box(tall, k, v[pl.ds(x * cy, cy), :], rows[:2], rows[2:])
     for s, d in sides(nx):
         rest.append(ex.start({"gx": d}, xsrc.at[pl.ds(1 + 2 * s, 2)], xh.at[pl.ds(2 * s, 2)]))
     for d in range(1, nx):
@@ -279,8 +281,8 @@
         qfw[k] = total_of(xzc) + (total_of(q, k) if k else 0.0)
         ends.append(pass_on(k, qfw.at[k], q))
 
-    gyc[...] = dot(split(ycar, 1), lower)
-    gyh[...] = dot(split(yh[...].reshape(4 * cx, cz), 1), band).reshape(4, cx, cz)
+    gyc[...] = dot(split(ycar, 1), w[:, pl.ds(0, cz)])
+    gyh[...] = dot(split(yh[...].reshape(4 * cx, cz), 1), w[:, pl.ds(cz, cz)]).reshape(4, cx, cz)
 
     def along_y(i):
         here = pl.ds(pl.multiple_of(i * PLANES, PLANES), PLANES)
@@ -400,6 +402,8 @@
         out_shape=[pltpu.VMEM(s, F32) for s in outs],
         scratch_shapes=[pltpu.VMEM(s, F32) for s in buffers]
         + [
+            pltpu.VMEM((2 * cz, 2 * cz), BF16),
+            pltpu.VMEM((5, 256, 128), BF16),
             pltpu.SemaphoreType.DMA((steps,)),
             pltpu.SemaphoreType.DMA((copies,)),
             pltpu.SemaphoreType.DMA((copies,)),

time: 17.7 us -> 17.2 us (0.972)
  Pallas kernels: 16.9 us -> 16.4 us
    pallas_call x1, Pallas kernels: 12.9 us -> 12.4 us  [per_device(): pl.pallas_call(functools.partial(exchange_kernel, cx, cy, cz), in_specs=[...]
where the time goes in v4:
time: 17.2 us; the launch traced here: 17 us
  Pallas kernels  16.4 us (95%)
  between operations  0.64 us (4%)
    pallas_call x1, Pallas kernels, per_device(): pl.pallas_call(functools.partial(exchange_kernel, cx, cy, cz), in_specs=[...  12.4 us
    pallas_call x1, Pallas kernels, per_device(): pl.pallas_call(functools.partial(final_kernel, cx, cy, cz, scale), in_spe...  3.97 us

profile of v4, /device:TPU:0, one launch (start us, length us, event | category | flops | bytes accessed | tf_op | source)
XLA Modules:
  0.0 17.0 jit_solution(18341657245763639290)
XLA Ops:
  0.6 12.4 %shard_map.30 = (f32[8192,128]{1,0:T(8,128)S(1)}, f32[8192,128]{1,0:T(8,128)S(1)}, f32[5,64,128]{2,1,0:T(8,128)S(1)}, f32[3,8,128]{2,1,0:T(8,128)S(1)}, f32[8,72,128]{2,1,0:T(8,128)S(1)}) custom-call(f32[8192,128]{1,0:T(8,128)} %bitcast.5), custom_call_target="tpu_custom_call" | custom-call | tf_op jit(solution)/shard_map/pallas_call | solution.py:398
  13.0 4.0 %shard_map.31 = (f32[8192,128]{1,0:T(8,128)}, f32[8192,128]{1,0:T(8,128)}) custom-call(f32[8192,128]{1,0:T(8,128)S(1)} %get-tuple-element.9.yp, f32[8192,128]{1,0:T(8,128)S(1)} %get-tuple-element.10.yb, f32[5,64,128]{2,1,0:T(8,128)S(1)} %get-tuple-element.11.xk, f32[3,8,128]{2,1,0:T(8,128)S(1)} %get-tuple-element.12.xe, f32[576,128]{1,0:T(8,128)S(1)} %bitcast.4), custom_call_target="tpu_custom_call" | custom-call | tf_op jit(solution)/shard_map/pallas_call | solution.py:417

commit v5 on v4

--- a/solution.py
+++ b/solution.py
@@ -168,7 +168,7 @@
         ref[...] = jnp.zeros_like(ref)
     barrier = pltpu.get_barrier_semaphore()
     near = [{"gy": d} for d in range(1, ny)] + [{"gx": d} for d in range(1, nx)]
-    near += [{"gz": d} for d in range(1, doublings(nz)[-1] + 1 if nz > 1 else 1)]
+    near += [{"gz": d} for d in range(1, nz)]
     near += [{"gx": d, "gz": e} for _, d in sides(nx) for _, e in sides(nz) if d > 0]
     peers = 0
     for shifts in near:
@@ -256,13 +256,13 @@
     rest, carries, ends = [], [], []
     if steps_z:
         carries.append(pass_on(0, zsrc.at[0], zc))
-    for s, d in sides(nz):
+    for s, d in sides(nz)[::-1]:
         rest.append(ex.start({"gz": d}, zsrc.at[pl.ds(1 + 2 * s, 2)], zh.at[pl.ds(2 * s, 2)]))
     xsrc[0] = y_prefix(xsum, jnp.sum(ycar, axis=0, keepdims=True))
     for k, x in enumerate((cx - 2, cx - 1, 0, 1)):
         rows = [yh[b, pl.ds(x, 1), :] for b in range(4)]
         xsrc[1 + k] = y_box(tall, k, v[pl.ds(x * cy, cy), :], rows[:2], rows[2:])
-    for s, d in sides(nx):
+    for s, d in sides(nx)[::-1]:
         rest.append(ex.start({"gx": d}, xsrc.at[pl.ds(1 + 2 * s, 2)], xh.at[pl.ds(2 * s, 2)]))
     for d in range(1, nx):
         rest.append(ex.start({"gx": d}, xsrc.at[0], xc.at[d - 1]))
@@ -276,10 +276,10 @@
         zfw[k] = zsrc[0] + total_of(zc, k)
         carries.append(pass_on(k, zfw.at[k], zc))
 
-    def forward_line(k):
-        arrived(ends[-1] if k else lines)
-        qfw[k] = total_of(xzc) + (total_of(q, k) if k else 0.0)
-        ends.append(pass_on(k, qfw.at[k], q))
+    def forward_line():
+        arrived(lines)
+        qfw[0] = total_of(xzc)
+        ends.append([ex.start({"gz": d}, qfw.at[0], q.at[d - 1]) for d in range(1, nz)])
 
     gyc[...] = dot(split(ycar, 1), w[:, pl.ds(0, cz)])
     gyh[...] = dot(split(yh[...].reshape(4 * cx, cz), 1), w[:, pl.ds(cz, cz)]).reshape(4, cx, cz)
@@ -296,8 +296,7 @@
 
     work = [functools.partial(pl.loop(early, steps), along_z)]
     work += [functools.partial(pl.loop(i, i + 2), along_y) for i in range(0, steps, 2)]
-    jobs = [functools.partial(forward_carry, k) for k in range(1, len(steps_z))]
-    jobs += [functools.partial(forward_line, k) for k in range(len(steps_z))]
+    jobs = [forward_line] + [functools.partial(forward_carry, k) for k in range(1, len(steps_z))]
     while work or jobs:
         if work:
             work.pop(0)()
@@ -393,7 +392,7 @@
         (5, arows, 128), (5, arows, 128), (8, 128), (4, 8, 128),
         (ly, cx, cz), (4, cx, cz), (ly, arows, 128), (2, 4, arows, 128),
         (lx, cy, cz), (4, cy, cz), (lz, arows, 128), (4, arows, 128),
-        (lx, 8, 128), (4, 8, 128), (lz, 8, 128), (lz, arows, 128), (lz, 8, 128), (cx, cz), (4, cx, cz), (4, cy + 16, cz),
+        (lx, 8, 128), (4, 8, 128), (max(nz - 1, 1), 8, 128), (lz, arows, 128), (1, 8, 128), (cx, cz), (4, cx, cz), (4, cy + 16, cz),
     ]
     yp, yb, xk, xe, zk = pl.pallas_call(
         functools.partial(exchange_kernel, cx, cy, cz),

time: 17.2 us -> 17 us (0.988)
  the two profiles are of different devices: /device:TPU:0 before, /device:TPU:5 now
where the time goes in v5:
time: 17 us; the launch traced here: 16.9 us
  Pallas kernels  16.2 us (95%)
  between operations  0.64 us (4%)
    pallas_call x1, Pallas kernels, per_device(): pl.pallas_call(functools.partial(exchange_kernel, cx, cy, cz), in_specs=[...  12.3 us
    pallas_call x1, Pallas kernels, per_device(): pl.pallas_call(functools.partial(final_kernel, cx, cy, cz, scale), in_spe...  3.97 us

profile of v5, /device:TPU:5, one launch (start us, length us, event | category | flops | bytes accessed | tf_op | source)
XLA Modules:
  0.0 16.9 jit_solution(15110066038614623523)
XLA Ops:
  0.6 12.3 %shard_map.30 = (f32[8192,128]{1,0:T(8,128)S(1)}, f32[8192,128]{1,0:T(8,128)S(1)}, f32[5,64,128]{2,1,0:T(8,128)S(1)}, f32[3,8,128]{2,1,0:T(8,128)S(1)}, f32[8,72,128]{2,1,0:T(8,128)S(1)}) custom-call(f32[8192,128]{1,0:T(8,128)} %bitcast.5), custom_call_target="tpu_custom_call" | custom-call | tf_op jit(solution)/shard_map/pallas_call | solution.py:397
  12.9 4.0 %shard_map.31 = (f32[8192,128]{1,0:T(8,128)}, f32[8192,128]{1,0:T(8,128)}) custom-call(f32[8192,128]{1,0:T(8,128)S(1)} %get-tuple-element.9.yp, f32[8192,128]{1,0:T(8,128)S(1)} %get-tuple-element.10.yb, f32[5,64,128]{2,1,0:T(8,128)S(1)} %get-tuple-element.11.xk, f32[3,8,128]{2,1,0:T(8,128)S(1)} %get-tuple-element.12.xe, f32[576,128]{1,0:T(8,128)S(1)} %bitcast.4), custom_call_target="tpu_custom_call" | custom-call | tf_op jit(solution)/shard_map/pallas_call | solution.py:416
